TPU v7x, 128 devices: a whole 4x4x4 slice. The times are simulated.
128 devices in a mesh: rep: 2 (over core), dp: 64 (over x, y, z).
Axes of the slice: x: 4, y: 4, z: 4, core: 2. Of those that a mesh axis runs over, the one named last changes fastest.
Arguments:
- g_w_gate: bfloat16 [128, 2, 896, 2560], P(('rep', 'dp')), parts along dimension 0
- g_w_up: bfloat16 [128, 2, 896, 2560], P(('rep', 'dp')), parts along dimension 0
- g_w_down: bfloat16 [128, 2, 2560, 896], P(('rep', 'dp')), parts along dimension 0
- w_gate: bfloat16 [2, 896, 2560], replicated
- w_up: bfloat16 [2, 896, 2560], replicated
- w_down: bfloat16 [2, 2560, 896], replicated
- m_w_gate: float32 [2, 896, 2560], P(None, 'dp')
- m_w_up: float32 [2, 896, 2560], P(None, 'dp')
- m_w_down: float32 [2, 2560, 896], P(None, 'dp')
- v_w_gate: float32 [2, 896, 2560], P(None, 'dp')
- v_w_up: float32 [2, 896, 2560], P(None, 'dp')
- v_w_down: float32 [2, 2560, 896], P(None, 'dp')
Outputs:
- output 1: bfloat16 [4, 896, 2560], P('rep'), parts along dimension 0
- output 2: bfloat16 [4, 896, 2560], P('rep'), parts along dimension 0
- output 3: bfloat16 [4, 2560, 896], P('rep'), parts along dimension 0
- output 4: float32 [4, 896, 2560], P('rep', 'dp'), parts along dimension 0
- output 5: float32 [4, 896, 2560], P('rep', 'dp'), parts along dimension 0
- output 6: float32 [4, 2560, 896], P('rep', 'dp'), parts along dimension 0
- output 7: float32 [4, 896, 2560], P('rep', 'dp'), parts along dimension 0
- output 8: float32 [4, 896, 2560], P('rep', 'dp'), parts along dimension 0
- output 9: float32 [4, 2560, 896], P('rep', 'dp'), parts along dimension 0
There are 2 independent parts. A program takes and returns all parts, laid end to end along the dimension named above; an argument that names none is the same for every part.
All inputs are finite; a program needn't handle non-finite values.
Results may differ from a plain program's by a relative error of at most 0.022.
Values are sent between devices in bfloat16 or wider.
A program may use at most 1.5 GiB of HBM per device.

v0:
```python
import jax
import jax.numpy as jnp
from jax import lax
from jax.sharding import PartitionSpec as P


def adamw(w, m, v, g):
    m = 0.9 * m + 0.1 * g
    v = 0.95 * v + 0.05 * g * g
    step = m * lax.rsqrt(v + 1e-8) + 0.1 * w
    return (w - 0.02 * step).astype(jnp.bfloat16), m, v


def clipped(gradients, sum_of_squares, count):
    factor = jnp.minimum(1.0, 0.5 * lax.rsqrt(sum_of_squares / count + 1e-30))
    return [g * factor for g in gradients]


def solution(mesh):
    def step(*arrays):
        terms, weights, m, v = (arrays[i : i + 3] for i in (0, 3, 6, 9))
        gradients = [lax.psum_scatter(t[0], "dp", scatter_dimension=1, tiled=True).astype(jnp.float32) for t in terms]
        squares = lax.psum(sum(jnp.sum(g * g) for g in gradients), "dp")
        gradients = clipped(gradients, squares, lax.psum(1, "dp") * sum(g.size for g in gradients))
        me = lax.axis_index("dp")
        own = [lax.dynamic_slice_in_dim(w, me * one.shape[1], one.shape[1], 1).astype(jnp.float32) for w, one in zip(weights, m, strict=True)]
        new = [adamw(w, m, v, g) for w, m, v, g in zip(own, m, v, gradients, strict=True)]
        whole = [lax.all_gather(one[0], "dp", axis=1, tiled=True) for one in new]
        return (*whole, *(one[1] for one in new), *(one[2] for one in new))

    all_of, cut = P(None, None, None), P(None, "dp", None)
    return jax.shard_map(
        step,
        mesh=mesh,
        in_specs=(P(("rep", "dp"), None, None, None),) * 3 + (all_of,) * 3 + (cut,) * 6,
        out_specs=(P("rep", None, None),) * 3 + (P("rep", "dp", None),) * 6,
        check_vma=False,
    )
```

profile of v0, /device:TPU:0, one launch (start us, length us, event | category | flops | bytes accessed | tf_op | source)
XLA Modules:
  0.0 1108.8 jit_solution(2503361154995392002)
XLA Ops:
  7.2 0.0 all-reduce.5.cloned.1.call-start
  7.2 0.0 copy-start
  7.2 39.3 %copy.48 = bf16[1,2,896,2560]{3,1,2,0:T(2,128)(2,1)} copy(bf16[1,2,896,2560]{3,2,1,0:T(8,128)(2,1)} %param.12) | data formatting | bytes 18350080 | tf_op args[0]
  46.5 0.0 copy-done
  46.5 26.1 %copy.47 = bf16[1,2,896,2560]{3,1,2,0:T(2,128)(2,1)} copy(bf16[1,2,896,2560]{3,2,1,0:T(8,128)(2,1)S(1)} %copy-done) | data formatting | bytes 18350080 | tf_op args[1]
  72.6 0.0 all-reduce.5.cloned.1.call-update
  72.6 0.0 reduce-scatter.4.cloned.1.call-start
  72.7 40.8 %copy.33 = bf16[2,2560,896]{2,0,1:T(2,128)(2,1)} copy(bf16[2,2560,896]{2,1,0:T(8,128)(2,1)} %bitcast.16) | data formatting | bytes 18350080
  113.5 8.8 copy.37
  122.3 0.0 copy-start.7
  122.3 0.0 copy-start.1
  122.3 0.0 copy-start.2
  122.3 0.0 copy-start.3
  122.3 0.0 copy-start.4
  122.3 0.0 copy-start.5
  122.3 0.0 copy-start.6
  122.3 0.0 reduce-scatter.4.cloned.1.call-update
  122.4 0.0 all-gather.4.cloned.1.call-start
  122.4 0.5 copy-done.7
  123.0 0.6 dynamic-slice
  124.2 174.8 %all-reduce.5.cloned.1.call-done = (bf16[2,896,2560]{2,0,1:T(2,128)(2,1)}, bf16[2,896,2560]{2,0,1:T(2,128)(2,1)}) async-done(((bf16[2,896,2560]{2,0,1:T(2,128)(2,1)}, bf16[2,896,2560]{2,0,1:T(2,128)(2,1)}), (bf16[2,896,2560]{2,0,1:T(2,128)(2,1)}, bf16[2,896,2560]{2,0,1:T(2,128)(2,1)})) %all-reduce.5.cloned.1.call-update) | async-done | bytes 18350096
  299.0 1.9 fusion.8
  302.2 370.2 %reduce-scatter.4.cloned.1.call-done = bf16[40,1792]{1,0:T(8,128)(2,1)} async-done(((bf16[2560,1792]{1,0:T(8,128)(2,1)}), bf16[40,1792]{1,0:T(8,128)(2,1)}) %reduce-scatter.4.cloned.1.call-update) | async-done | bytes 143376
  672.3 0.9 reshape.19
  673.3 0.7 fusion.10
  674.6 1.2 constant_dynamic-slice_fusion
  675.8 172.6 %psum.7 = f32[]{:T(128)} all-reduce(f32[]{:T(128)S(6)} %add.65), channel_id=1, replica_groups=mesh['rep'=2,'dp'=64] {'dp'}, use_global_device_ids=true, to_apply=%region_6.0 | all-reduce | flops 1 | bytes 8 | tf_op jit(solution)/shard_map/psum | solution.py:23
  849.1 0.0 copy-done.1
  849.1 0.0 copy-done.2
  849.1 2.5 fusion.19
  851.7 0.0 all-gather.4.cloned.1.call-update
  851.7 0.0 all-gather.6.cloned.1.call-start
  851.8 0.0 copy-done.3
  851.8 0.0 copy-done.4
  851.8 2.5 fusion.20
  854.3 0.0 all-gather.6.cloned.1.call-update
  854.3 0.2 all-gather.8.cloned.1.call-start
  854.6 0.0 copy-done.5
  854.6 0.0 copy-done.6
  854.6 1.8 fusion.15
  856.4 0.0 all-gather.8.cloned.1.call-update
  856.5 70.8 %all-gather.4.cloned.1.call-done = bf16[2,896,2560]{2,0,1:T(2,128)(2,1)} async-done(((bf16[2,14,2560]{2,0,1:T(2,128)(2,1)}), bf16[2,896,2560]{2,0,1:T(2,128)(2,1)}) %all-gather.4.cloned.1.call-update) | async-done | bytes 9175056 | tf_op jit(solution)/shard_map/all_gather | solution.py:28
  927.3 8.7 copy.31
  936.0 74.8 %all-gather.6.cloned.1.call-done = bf16[2,896,2560]{2,0,1:T(2,128)(2,1)} async-done(((bf16[2,14,2560]{2,0,1:T(2,128)(2,1)}), bf16[2,896,2560]{2,0,1:T(2,128)(2,1)}) %all-gather.6.cloned.1.call-update) | async-done | bytes 9175056 | tf_op jit(solution)/shard_map/all_gather | solution.py:28
  1010.8 8.7 copy.32
  1019.4 74.8 %all-gather.8.cloned.1.call-done = bf16[2,2560,896]{2,1,0:T(8,128)(2,1)} async-done(((bf16[2,40,896]{2,1,0:T(8,128)(2,1)}), bf16[2,2560,896]{2,1,0:T(8,128)(2,1)}) %all-gather.8.cloned.1.call-update) | async-done | bytes 9175056 | tf_op jit(solution)/shard_map/all_gather | solution.py:28
  1094.3 8.0 copy.52
Async XLA Ops:
  7.2 291.8 %all-reduce.5.cloned.1.call-start = ((), (), s32[]{:S(2)}) async-start(), calls=%async_computation.5 | async-start | bytes 36700160
  7.2 39.3 %copy-start = (bf16[1,2,896,2560]{3,2,1,0:T(8,128)(2,1)S(1)}, bf16[1,2,896,2560]{3,2,1,0:T(8,128)(2,1)}, u32[]{:S(2)}) copy-start(bf16[1,2,896,2560]{3,2,1,0:T(8,128)(2,1)} %param.13) | copy-start | bytes 27525124
  72.6 599.7 %reduce-scatter.4.cloned.1.call-start = ((), (), s32[]{:S(2)}) async-start(), calls=%async_computation.4 | async-start | bytes 9318400
  122.3 0.7 copy-start.7
  122.3 726.8 %copy-start.1 = (f32[2,14,2560]{2,0,1:T(2,128)S(1)}, f32[2,14,2560]{2,0,1:T(2,128)}, u32[]{:S(2)}) copy-start(f32[2,14,2560]{2,0,1:T(2,128)} %param.21) | copy-start | bytes 860164
  122.3 726.8 %copy-start.2 = (f32[2,14,2560]{2,0,1:T(2,128)S(1)}, f32[2,14,2560]{2,0,1:T(2,128)}, u32[]{:S(2)}) copy-start(f32[2,14,2560]{2,0,1:T(2,128)} %param.18) | copy-start | bytes 860164
  122.3 729.4 %copy-start.3 = (f32[2,14,2560]{2,0,1:T(2,128)S(1)}, f32[2,14,2560]{2,0,1:T(2,128)}, u32[]{:S(2)}) copy-start(f32[2,14,2560]{2,0,1:T(2,128)} %param.22) | copy-start | bytes 860164
  122.3 729.5 %copy-start.4 = (f32[2,14,2560]{2,0,1:T(2,128)S(1)}, f32[2,14,2560]{2,0,1:T(2,128)}, u32[]{:S(2)}) copy-start(f32[2,14,2560]{2,0,1:T(2,128)} %param.19) | copy-start | bytes 860164
  122.3 732.3 %copy-start.5 = (f32[2,40,896]{2,1,0:T(8,128)S(1)}, f32[2,40,896]{2,1,0:T(8,128)}, u32[]{:S(2)}) copy-start(f32[2,40,896]{2,1,0:T(8,128)} %param.23) | copy-start | bytes 860164
  122.3 732.3 %copy-start.6 = (f32[2,40,896]{2,1,0:T(8,128)S(1)}, f32[2,40,896]{2,1,0:T(8,128)}, u32[]{:S(2)}) copy-start(f32[2,40,896]{2,1,0:T(8,128)} %param.20) | copy-start | bytes 860164
  122.4 804.9 %all-gather.4.cloned.1.call-start = ((), (), s32[]{:S(2)}) async-start(), calls=%async_computation.1 | async-start | bytes 9318400 | tf_op jit(solution)/shard_map/all_gather | solution.py:28
  851.7 159.1 %all-gather.6.cloned.1.call-start = ((), (), s32[]{:S(2)}) async-start(), calls=%async_computation.2 | async-start | bytes 9318400 | tf_op jit(solution)/shard_map/all_gather | solution.py:28
  854.3 239.9 %all-gather.8.cloned.1.call-start = ((), (), s32[]{:S(2)}) async-start(), calls=%async_computation.3 | async-start | bytes 9318400 | tf_op jit(solution)/shard_map/all_gather | solution.py:28
Sparse Core Ops, SparseCore 0:
  72.8 226.1 all-reduce.4
  301.4 370.9 reduce-scatter.3
  851.8 75.4 all-gather.3
  930.6 80.1 all-gather.5
  1013.5 80.7 all-gather.7
where the time goes:
time: 1110 us
  waiting for transfers between devices  765 us (69%)
  blocking collectives  173 us (16%)
  local copies, waits for them, and re-layouts  144 us (13%)
  between operations  17.2 us (2%)
    unnamed x7, waiting for transfers between devices  545 us
    all_gather x3, waiting for transfers between devices, step(): whole = [lax.all_gather(one[0], 'dp', axis=1, tiled=True) for one in new]  220 us
    psum x1, blocking collectives, step(): squares = lax.psum(sum((jnp.sum(g * g) for g in gradients)), 'dp')  173 us
    unnamed x25, local copies, waits for them, and re-layouts  142 us
  transfers between devices with their start and end apart: 5, of which 5 were waited for; matrix products, arithmetic and copies ran while one was open for 7% of the time, Pallas kernels for 0%

commit v1 on v0

v1 whole, which is shorter than its diff:
```python
import functools

import jax
import jax.numpy as jnp
from jax import lax
from jax.experimental import pallas as pl
from jax.experimental.pallas import tpu as pltpu
from jax.sharding import PartitionSpec as P

MESH = pl.DeviceIdType.MESH
F32, BF16 = jnp.float32, jnp.bfloat16
ROWS, PAD = 14, 16
BLOCK, TALL = 4 * ROWS, 40
STRIDE = (16, 4, 1)
X, Y, Z = GATE, UP, DOWN = range(3)
PAIR = (0, 1)
ALL = slice(None)
VMEM_LIMIT = 58 * 1024 * 1024


def place():
    me = lax.axis_index("dp")
    c = (lax.div(me, 16), lax.rem(lax.div(me, 4), 4), lax.rem(me, 4))

    def peer(axis, shift):
        return me + (lax.rem(c[axis] + (shift % 4), 4) - c[axis]) * STRIDE[axis]

    return c, peer


def mod4(value):
    return lax.rem(value + 8, 4)


def greet(peers):
    barrier = pltpu.get_barrier_semaphore()
    for p in peers:
        pl.semaphore_signal(barrier, inc=1, device_id={"dp": p}, device_id_type=MESH)
    pl.semaphore_wait(barrier, len(peers))


def tiles(shape, body):
    if len(shape) == 3:
        @pl.loop(0, shape[0])
        def _(i):
            body((i, ALL, ALL))
    elif shape[0] == TALL:
        body((ALL, ALL))
    else:
        width = next(w for w in (512, 256, 128) if shape[1] % w == 0)
        @pl.loop(0, shape[1] // width)
        def _(i):
            body((ALL, pl.ds(pl.multiple_of(i * width, width), width)))


class Copies:
    def __init__(self, send, recv):
        self.send, self.recv, self.next, self.made = send, recv, 0, []

    def remote(self, src, dst, device):
        n = self.next
        self.next += 1
        copy = pltpu.make_async_remote_copy(
            src_ref=src, dst_ref=dst, send_sem=self.send.at[n], recv_sem=self.recv.at[n],
            device_id={"dp": device}, device_id_type=MESH,
        )
        self.made.append(copy)
        return copy

    def drain(self):
        for copy in self.made:
            copy.wait_send()


class Local:
    def __init__(self, sem):
        self.sem, self.next = sem, 0

    def start(self, src, dst):
        copy = pltpu.make_async_copy(src, dst, self.sem.at[self.next])
        self.next += 1
        copy.start()
        return copy


def scatter_kernel(cols, fcols, count, *refs):
    it = iter(refs)
    take = lambda n: [next(it) for _ in range(n)]
    three = lambda: take(3)
    g, w, m, v = three(), three(), three(), three()
    new_w, new_m, new_v = three(), three(), three()
    own1, ro1, rd1, rs1 = three(), three(), three(), three()
    sb2, sf2, ro2, rd2, rs2 = three(), three(), three(), three(), three()
    sb3, sf3, ro3, rd3, rs3 = three(), three(), three(), three(), three()
    fold, four, raw_w, raw_m, raw_v, w32, m32, v32, gf = take(9)
    wd, md, vd, gd = take(4)
    part, parts = take(2)
    send, recv, lsem = three()
    (x, y, z), peer = place()
    c = (x, y, z)
    copies, local = Copies(send, recv), Local(lsem)
    AXES = ((X, Y, Z), (Y, Z, X), (Z, X, Y))
    JAXIS = (Y, X, X)
    SIGN = (1, -1)

    def order(axis, layer):
        s = SIGN[layer]
        return [mod4(c[axis] + d) for d in (2, -s, s, 0)]

    def unit(a, layer, k, j):
        if a == GATE:
            return g[GATE].at[layer, k, j]
        if a == UP:
            return g[UP].at[layer, j, k]
        return g[DOWN].at[layer, j, :, k]

    everyone = [peer(axis, shift) for axis in (X, Y, Z) for shift in (1, 2, 3)]

    small = [local.start(m[a], dst) for a, dst in ((0, raw_m.at[0]), (1, raw_m.at[1]), (2, md))]
    small += [local.start(v[a], dst) for a, dst in ((0, raw_v.at[0]), (1, raw_v.at[1]), (2, vd))]
    small += [local.start(w[a].at[:, x, y], raw_w.at[a]) for a in (0, 1)]
    small += [local.start(w[DOWN].at[:, x, y, z], wd)]

    greet(everyone)

    opp1, dir1, own_s = {}, {}, {}
    for p in range(4):
        for a in range(3):
            for layer in PAIR:
                ax, s, j = AXES[a][0], SIGN[layer], order(JAXIS[a], layer)[p]
                copy = copies.remote(unit(a, layer, mod4(c[ax] + 2), j), ro1[a].at[layer, p], peer(ax, s))
                copy.start()
                opp1[a, layer, p] = copy
                own_s[a, layer, p] = local.start(unit(a, layer, mod4(c[ax] + s), j), own1[a].at[layer, p])
    for p in range(4):
        for a in range(3):
            for layer in PAIR:
                ax, s, j = AXES[a][0], SIGN[layer], order(JAXIS[a], layer)[p]
                copy = copies.remote(unit(a, layer, mod4(c[ax] - s), j), rd1[a].at[layer, p], peer(ax, -s))
                copy.start()
                dir1[a, layer, p] = copy

    fold[BLOCK:64, :] = jnp.zeros((8, cols), F32)

    def part_of(value, at, which):
        fold[(slice(0, BLOCK), at)] = value
        for k in range(4):
            four[(k, ALL, at)] = fold[(slice(k * ROWS, k * ROWS + PAD), at)]
        return [four[(k, ALL, at)] for k in which]

    for copy in small:
        copy.wait()
    for src, dst in ((raw_m, m32), (raw_v, v32)):
        for a in PAIR:
            @pl.loop(0, ROWS)
            def _(r):
                pair = src[a, r]
                dst[a, 0, pl.ds(r, 1), :] = pair[0:1, :]
                dst[a, 1, pl.ds(r, 1), :] = pair[1:2, :]
    for a in PAIR:
        for layer in PAIR:
            def widen(index):
                w32[(a, layer, ALL, index[1])] = part_of(raw_w[(a, layer, *index)].astype(F32), index[1], [z])[0]
            tiles((BLOCK, cols), widen)

    def add(dst, one, two):
        def body(index):
            dst[index] = (one[index].astype(F32) + two[index].astype(F32)).astype(BF16)
        tiles(one.shape, body)

    sum1, own_f = {}, {}
    for p in range(4):
        for a in range(3):
            for layer in PAIR:
                ax, s, j = AXES[a][0], SIGN[layer], order(JAXIS[a], layer)[p]
                opp1[a, layer, p].wait_recv()
                own_s[a, layer, p].wait()
                here = ro1[a].at[layer, p]
                add(here, here, own1[a].at[layer, p])
                copy = copies.remote(here, rs1[a].at[layer, p], peer(ax, s))
                copy.start()
                sum1[a, layer, p] = copy
                own_f[a, layer, p] = local.start(unit(a, layer, c[ax], j), own1[a].at[layer, p])

    def total(one, two, three, index):
        return one[index].astype(F32) + two[index].astype(F32) + three[index].astype(F32)

    def cut(one, two, three, layer, sb, sf):
        pieces = order(Z, layer)

        def body(index):
            at = index[1]
            for role, piece in enumerate(part_of(total(one, two, three, index), at, pieces)):
                if role < 2:
                    sb[(role, ALL, at)] = piece.astype(BF16)
                else:
                    sf[(role - 2, ALL, at)] = piece
        tiles((BLOCK, cols), body)

    opp2, dir2 = {}, {}

    def send2(a, layer, role, src, key):
        ax, s = AXES[a][1], SIGN[layer]
        if role == 0:
            copy = copies.remote(src, ro2[a].at[key], peer(ax, s))
            opp2[(a, *key)] = copy
        else:
            copy = copies.remote(src, rd2[a].at[key], peer(ax, -s))
            dir2[(a, *key)] = copy
        copy.start()

    for p in range(4):
        for a in range(3):
            for layer in PAIR:
                sum1[a, layer, p].wait_recv()
                dir1[a, layer, p].wait_recv()
                own_f[a, layer, p].wait()
                one, two, three = own1[a].at[layer, p], rs1[a].at[layer, p], rd1[a].at[layer, p]
                if a == UP:
                    cut(one, two, three, layer, sb2[UP].at[layer, p], sf2[UP].at[layer, p])
                    send2(1, layer, 0, sb2[UP].at[layer, p, 0], (layer, p))
                    send2(1, layer, 1, sb2[UP].at[layer, p, 1], (layer, p))
                    continue

                def body(index, one=one, two=two, three=three, a=a, layer=layer, p=p):
                    value = total(one, two, three, index)
                    if p < 2:
                        sb2[a][(layer, p, *index)] = value.astype(BF16)
                    else:
                        sf2[a][(layer, p - 2, *index)] = value
                tiles(one.shape, body)
                if p < 2:
                    send2(a, layer, p, sb2[a].at[layer, p], (layer,))

    sum2 = {}

    def pass2(a, layer, key, own):
        opp2[(a, *key)].wait_recv()
        here = ro2[a].at[key]
        add(here, here, own)
        copy = copies.remote(here, rs2[a].at[key], peer(AXES[a][1], SIGN[layer]))
        copy.start()
        sum2[(a, *key)] = copy

    for a in (0, 2):
        for layer in PAIR:
            pass2(a, layer, (layer,), sf2[a].at[layer, 0])
    for p in range(4):
        for layer in PAIR:
            pass2(1, layer, (layer, p), sf2[UP].at[layer, p, 0])

    opp3, dir3, sum3 = {}, {}, {}

    def send3(a, layer, role):
        ax, s = AXES[a][2], SIGN[layer]
        if role == 0:
            opp3[a, layer] = copy = copies.remote(sb3[a].at[layer, 0], ro3[a].at[layer], peer(ax, s))
        else:
            dir3[a, layer] = copy = copies.remote(sb3[a].at[layer, 1], rd3[a].at[layer], peer(ax, -s))
        copy.start()

    for layer in PAIR:
        sum2[0, layer].wait_recv()
        dir2[0, layer].wait_recv()
        cut(sf2[GATE].at[layer, 1], rs2[GATE].at[layer], rd2[GATE].at[layer], layer, sb3[GATE].at[layer], sf3[GATE].at[layer])
        send3(0, layer, 0)
        send3(0, layer, 1)
    for layer in PAIR:
        sum2[2, layer].wait_recv()
        dir2[2, layer].wait_recv()
        for role, k in enumerate(order(Y, layer)):
            value = total(sf2[DOWN].at[layer, 1], rs2[DOWN].at[layer], rd2[DOWN].at[layer], (k, ALL, ALL))
            if role < 2:
                sb3[DOWN][layer, role] = value.astype(BF16)
                send3(2, layer, role)
            else:
                sf3[DOWN][layer, role - 2] = value
    for p in range(4):
        for layer in PAIR:
            sum2[1, layer, p].wait_recv()
            dir2[1, layer, p].wait_recv()

            def body(index, layer=layer, p=p):
                value = total(sf2[UP].at[layer, p, 1], rs2[UP].at[layer, p], rd2[UP].at[layer, p], index)
                if p < 2:
                    sb3[UP][(layer, p, *index)] = value.astype(BF16)
                else:
                    sf3[UP][(layer, p - 2, *index)] = value
            tiles((PAD, cols), body)
            if p < 2:
                send3(1, layer, p)

    for a in (0, 2, 1):
        for layer in PAIR:
            opp3[a, layer].wait_recv()
            here = ro3[a].at[layer]
            add(here, here, sf3[a].at[layer, 0])
            sum3[a, layer] = copy = copies.remote(here, rs3[a].at[layer], peer(AXES[a][2], SIGN[layer]))
            copy.start()

    part[...] = jnp.zeros((8, 128), F32)

    def square(value):
        rows, width = value.shape
        value = value * value
        lines = sum(value[r : r + 8] for r in range(0, rows, 8))
        return sum(lines[:, k : k + 128] for k in range(0, width, 128))

    for a in (0, 2, 1):
        for layer in PAIR:
            sum3[a, layer].wait_recv()
            dir3[a, layer].wait_recv()

            def body(index, a=a, layer=layer):
                value = total(sf3[a].at[layer, 1], rs3[a].at[layer], rd3[a].at[layer], index)
                value = value.astype(BF16).astype(F32)
                if a == DOWN:
                    gd[(layer, *index)] = value
                else:
                    value = jnp.where(lax.broadcasted_iota(jnp.int32, value.shape, 0) < ROWS, value, 0.0)
                    gf[(a, layer, *index)] = value
                part[...] += square(value)
            tiles((TALL, fcols) if a == DOWN else (PAD, cols), body)

    value = part[...]
    for axis in (X, Y, Z):
        mine = parts.at[axis, c[axis]]
        mine[...] = value
        line = [copies.remote(mine, mine, peer(axis, shift)) for shift in (1, 2, 3)]
        for copy in line:
            copy.start()
        for copy in line:
            copy.wait_recv()
        value = (parts[axis, 0] + parts[axis, 1]) + (parts[axis, 2] + parts[axis, 3])
    squares = jnp.full((8, 128), jnp.sum(value), F32)
    factor = jnp.minimum(1.0, 0.5 * lax.rsqrt(squares / count + 1e-30))[0:1, 0:1]

    def adamw(ww, mm, vv, gg):
        gg = gg * factor
        mm = 0.9 * mm + 0.1 * gg
        vv = 0.95 * vv + 0.05 * gg * gg
        step = mm * lax.rsqrt(vv + 1e-8) + 0.1 * ww
        return (ww - 0.02 * step).astype(BF16), mm, vv

    for a in PAIR:
        for layer in PAIR:
            def body(index, a=a, layer=layer):
                at = (a, layer, *index)
                out = (layer, *index)
                new_w[a][out], new_m[a][out], new_v[a][out] = adamw(w32[at], m32[at], v32[at], gf[at])
            tiles((PAD, cols), body)
    for layer in PAIR:
        new_w[DOWN][layer], new_m[DOWN][layer], new_v[DOWN][layer] = adamw(wd[layer].astype(F32), md[layer], vd[layer], gd[layer])
    copies.drain()


def gather_kernel(cols, fcols, *refs):
    it = iter(refs)
    take = lambda n: [next(it) for _ in range(n)]
    three = lambda: take(3)
    own, out = three(), three()
    first, second, fold, send, recv = take(5)
    (x, y, z), peer = place()
    c = (x, y, z)
    copies = Copies(send, recv)
    greet([peer(axis, shift) for axis in (X, Y, Z) for shift in (1, 3)])

    class Ring:
        def __init__(self, axis, slot, source=None):
            self.axis, self.slot = axis, slot
            k = c[axis]
            self.left, self.right = mod4(k - 1), mod4(k + 1)
            self.arrive, self.onward = {}, {}
            for layer in PAIR:
                for side in (1, -1):
                    copy = copies.remote((source or slot)(layer, k), slot(layer, k), peer(axis, side))
                    copy.start()
                    self.arrive[layer, side] = copy

        def forward(self):
            for layer, side, k in ((0, 1, self.left), (1, -1, self.right)):
                self.arrive[layer, side].wait_recv()
                self.onward[layer] = copy = copies.remote(self.slot(layer, k), self.slot(layer, k), peer(self.axis, side))
                copy.start()

        def near(self):
            self.arrive[1, 1].wait_recv()
            self.arrive[0, -1].wait_recv()

        def far(self):
            self.onward[0].wait_recv()
            self.onward[1].wait_recv()

    gate1 = Ring(Z, lambda layer, k: first.at[layer, k], lambda layer, k: own[GATE].at[layer])
    up1 = Ring(X, lambda layer, k: second.at[layer, k, z], lambda layer, k: own[UP].at[layer])
    down1 = Ring(Y, lambda layer, k: out[DOWN].at[layer, x, k, z], lambda layer, k: own[DOWN].at[layer])
    for layer in PAIR:
        first[layer, z] = own[GATE][layer]
        second[layer, x, z] = own[UP][layer]
        out[DOWN][layer, x, y, z] = own[DOWN][layer]

    def up_unit(xb):
        return Ring(Z, lambda layer, k: second.at[layer, xb, k])

    def down_unit(yb):
        return Ring(X, lambda layer, k: out[DOWN].at[layer, k, yb, z])

    def compact(pieces, dst):
        def body(index):
            at = index[1]
            for k in range(4):
                fold[(pl.ds(k * ROWS, PAD), at)] = pieces[(k, ALL, at)].astype(F32)
            dst[(ALL, at)] = fold[(slice(0, BLOCK), at)].astype(BF16)
        tiles((BLOCK, cols), body)

    gate1.forward()
    up1.forward()
    down1.forward()
    up2, down2 = [up_unit(x)], [down_unit(y)]
    gate1.near()
    gate1.far()
    for layer in PAIR:
        compact(first.at[layer], out[GATE].at[layer, x, y])
    gate2 = Ring(Y, lambda layer, k: out[GATE].at[layer, x, k])

    def gate_unit(yb):
        return Ring(X, lambda layer, k: out[GATE].at[layer, k, yb])

    def up_last(xb):
        for layer in PAIR:
            compact(second.at[layer, xb], out[UP].at[layer, xb, y])
        return Ring(Y, lambda layer, k: out[UP].at[layer, xb, k])

    def down_last(xb):
        return Ring(Z, lambda layer, k: out[DOWN].at[layer, xb, :, k])

    up1.near()
    down1.near()
    up2 += [up_unit(mod4(x - 1)), up_unit(mod4(x + 1))]
    down2 += [down_unit(mod4(y - 1)), down_unit(mod4(y + 1))]
    up1.far()
    down1.far()
    up2 += [up_unit(mod4(x + 2))]
    down2 += [down_unit(mod4(y + 2))]
    gate3 = [gate_unit(y)]
    down3 = [down_last(x)]
    for ring in up2 + down2:
        ring.forward()
    gate2.forward()
    up2[0].near()
    up2[0].far()
    up3 = [up_last(x)]
    gate2.near()
    gate3 += [gate_unit(mod4(y - 1)), gate_unit(mod4(y + 1))]
    for ring in down2:
        ring.near()
    down3 += [down_last(mod4(x - 1)), down_last(mod4(x + 1))]
    for ring, xb in zip(up2[1:], (mod4(x - 1), mod4(x + 1), mod4(x + 2))):
        ring.near()
        ring.far()
        up3.append(up_last(xb))
    gate2.far()
    gate3.append(gate_unit(mod4(y + 2)))
    for ring in down2:
        ring.far()
    down3.append(down_last(mod4(x + 2)))
    for rings in zip(gate3, up3, down3):
        for ring in rings:
            ring.forward()
    for rings in zip(gate3, up3, down3):
        for ring in rings:
            ring.near()
            ring.far()
    copies.drain()


def write_kernel(*refs):
    it = iter(refs)
    take = lambda n: [next(it) for _ in range(n)]
    three = lambda: take(3)
    w, m, v = three(), three(), three()
    out_w, out_m, out_v = three(), three(), three()
    pairs, sem = take(2)
    local = Local(sem)
    copies = [local.start(w[a].at[layer, xb], out_w[a].at[layer, xb]) for a in range(3) for layer in (0, 1) for xb in range(4)]
    copies += [local.start(m[DOWN], out_m[DOWN]), local.start(v[DOWN], out_v[DOWN])]
    for n, (src, dst) in enumerate(((m[GATE], out_m[GATE]), (m[UP], out_m[UP]), (v[GATE], out_v[GATE]), (v[UP], out_v[UP]))):
        @pl.loop(0, ROWS)
        def _(r):
            for layer in PAIR:
                pairs[n, r, layer : layer + 1, :] = src[layer, pl.ds(r, 1), :]
        copies.append(local.start(pairs.at[n], dst))
    for copy in copies:
        copy.wait()


def solution(mesh):
    def step(*arrays):
        terms, weights, m, v = (arrays[i : i + 3] for i in (0, 3, 6, 9))
        cols, fcols = terms[0].shape[-1], terms[2].shape[-1]
        rows, frows = terms[0].shape[-2], terms[2].shape[-2]
        assert rows == 64 * ROWS and frows == 64 * TALL
        wide = lambda t: t.reshape(2, 4, 4, 4 * ROWS, cols)
        tall = lambda t: t.reshape(2, 4, 4, 4, TALL, fcols)
        shaped = lambda three: (wide(three[0]), wide(three[1]), tall(three[2]))
        turned = lambda three: (three[0].transpose(1, 0, 2), three[1].transpose(1, 0, 2), three[2])
        count = 2 * (2 * rows * cols + frows * fcols)
        anywhere, on_chip = pl.BlockSpec(memory_space=pl.ANY), pl.BlockSpec(memory_space=pltpu.VMEM)
        B, F = (lambda *shape: pltpu.VMEM(shape, BF16)), (lambda *shape: pltpu.VMEM(shape, F32))
        unit1 = ((BLOCK, cols), (BLOCK, cols), (4, TALL, fcols))
        unit2 = ((2, BLOCK, cols), (2, 4, PAD, cols), (2, 4, TALL, fcols))
        two2 = ((2, 2, BLOCK, cols), (2, 4, 2, PAD, cols), (2, 2, 4, TALL, fcols))
        unit3 = ((PAD, cols), (PAD, cols), (TALL, fcols))
        scratch = [B(2, 4, *u) for _ in range(4) for u in unit1]
        scratch += [B(*u) for u in two2] + [F(*u) for u in two2]
        scratch += [B(*u) for _ in range(3) for u in unit2]
        scratch += [B(2, 2, *u) for u in unit3] + [F(2, 2, *u) for u in unit3]
        scratch += [B(2, *u) for _ in range(3) for u in unit3]
        scratch += [F(64, cols), F(4, PAD, cols), B(2, 2, BLOCK, cols), F(2, ROWS, 2, cols), F(2, ROWS, 2, cols)]
        scratch += [F(2, 2, PAD, cols)] * 4
        scratch += [B(2, TALL, fcols), F(2, TALL, fcols), F(2, TALL, fcols), F(2, TALL, fcols)]
        scratch += [F(8, 128), F(3, 4, 8, 128)]
        scratch += [pltpu.SemaphoreType.DMA((135,)), pltpu.SemaphoreType.DMA((135,)), pltpu.SemaphoreType.DMA((57,))]
        small = [(2, PAD, cols), (2, PAD, cols), (2, TALL, fcols)]
        made = pl.pallas_call(
            functools.partial(scatter_kernel, cols, fcols, count),
            out_shape=[pltpu.VMEM(s, BF16) for s in small] + [pltpu.VMEM(s, F32) for s in small * 2],
            in_specs=[anywhere] * 12,
            out_specs=[on_chip] * 9,
            scratch_shapes=scratch,
            compiler_params=pltpu.CompilerParams(collective_id=0, has_side_effects=True, vmem_limit_bytes=VMEM_LIMIT),
            name="scatter",
        )(*shaped([t[0] for t in terms]), *shaped(weights), *turned(m), *turned(v))
        big = [(2, 4, 4, BLOCK, cols), (2, 4, 4, BLOCK, cols), (2, 4, 4, 4, TALL, fcols)]
        whole = pl.pallas_call(
            functools.partial(gather_kernel, cols, fcols),
            out_shape=[pltpu.VMEM(s, BF16) for s in big],
            in_specs=[on_chip] * 3,
            out_specs=[on_chip] * 3,
            scratch_shapes=[B(2, 4, PAD, cols), B(2, 4, 4, PAD, cols), F(64, cols), pltpu.SemaphoreType.DMA((144,)), pltpu.SemaphoreType.DMA((144,))],
            compiler_params=pltpu.CompilerParams(collective_id=1, has_side_effects=True, vmem_limit_bytes=16 * 1024 * 1024),
            name="gather",
        )(*made[:3])
        turned_small = [(ROWS, 2, cols), (ROWS, 2, cols), (2, TALL, fcols)]
        outs = pl.pallas_call(
            write_kernel,
            out_shape=[jax.ShapeDtypeStruct(s, BF16) for s in big] + [jax.ShapeDtypeStruct(s, F32) for s in turned_small * 2],
            in_specs=[on_chip] * 9,
            out_specs=[anywhere] * 9,
            scratch_shapes=[F(4, ROWS, 2, cols), pltpu.SemaphoreType.DMA((30,))],
            compiler_params=pltpu.CompilerParams(vmem_limit_bytes=16 * 1024 * 1024),
            name="write",
        )(*whole, *made[3:])
        back = lambda three: tuple(t.transpose(1, 0, 2) for t in three[:2]) + (three[2],)
        news = tuple(one.reshape(w.shape) for one, w in zip(outs[:3], weights, strict=True))
        return (*news, *back(outs[3:6]), *back(outs[6:9]))

    all_of, cut = P(None, None, None), P(None, "dp", None)
    return jax.shard_map(
        step,
        mesh=mesh,
        in_specs=(P(("rep", "dp"), None, None, None),) * 3 + (all_of,) * 3 + (cut,) * 6,
        out_specs=(P("rep", None, None),) * 3 + (P("rep", "dp", None),) * 6,
        check_vma=False,
    )
```

time: 1110 us -> 245 us (0.22)
  waiting for transfers between devices: 765 us -> 0 us
  Pallas kernels: 0 us -> 244 us
  blocking collectives: 173 us -> 0 us
  local copies, waits for them, and re-layouts: 144 us -> 0 us
  between operations: 17.2 us -> 0.66 us
    unnamed x7 -> x0, waiting for transfers between devices: 545 us -> none
    pallas_call x0 -> x3, Pallas kernels: none -> 244 us  [the longest x1 126 us: step(): pl.pallas_call(functools.partial(scatter_kernel, cols, fcols, count), out...]
    all_gather x3 -> x0, waiting for transfers between devices: 220 us -> none  [step(): whole = [lax.all_gather(one[0], 'dp', axis=1, tiled=True) for one in new]]
    psum x1 -> x0, blocking collectives: 173 us -> none  [step(): squares = lax.psum(sum((jnp.sum(g * g) for g in gradients)), 'dp')]
    unnamed x25 -> x0, local copies, waits for them, and re-layouts: 142 us -> none
  transfers between devices with their start and end apart: 5 -> 0, of which waited for: 5 -> 0; matrix products, arithmetic and copies ran while one was open for 7% -> 0% of each run, Pallas kernels for 0% -> 0%
where the time goes in v1:
time: 245 us
  Pallas kernels  244 us (100%)
    pallas_call x1, Pallas kernels, step(): pl.pallas_call(functools.partial(scatter_kernel, cols, fcols, count), out...  126 us
    pallas_call x1, Pallas kernels, step(): pl.pallas_call(functools.partial(gather_kernel, cols, fcols), out_shape=[...  109 us
    pallas_call x1, Pallas kernels, step(): pl.pallas_call(write_kernel, out_shape=[jax.ShapeDtypeStruct(s, BF16) for...  9.82 us

profile of v1, /device:TPU:0, one launch (start us, length us, event | category | flops | bytes accessed | tf_op | source)
XLA Modules:
  0.0 244.8 jit_solution(15173217965729171731)
XLA Ops:
  0.6 125.7 %scatter.1 = (bf16[2,16,2560]{2,1,0:T(8,128)(2,1)S(1)}, bf16[2,16,2560]{2,1,0:T(8,128)(2,1)S(1)}, bf16[2,40,896]{2,1,0:T(8,128)(2,1)S(1)}, f32[2,16,2560]{2,1,0:...) custom-call(bf16[2,4,4,56,2560]{4,3,2,1,0:T(8,128)(2,1)} %bitcast.17, ...), custom_call_target="tpu_custom_call" | custom-call | tf_op jit(solution)/shard_map/scatter/pallas_call | solution.py:525
  126.3 108.7 %gather.1 = (bf16[2,4,4,56,2560]{4,3,2,1,0:T(8,128)(2,1)S(1)}, bf16[2,4,4,56,2560]{4,3,2,1,0:T(8,128)(2,1)S(1)}, bf16[2,4,4,4,40,896]{5,4,3,2,1,0:T(8,128)(2,1)S(1)}) custom-call(bf16[2,16,2560]{2,1,0:T(8,128)(2,1)S(1)} %get-tuple-element.30.refs_0_, bf16[2,16,2560]{2,1,0:T(8,128)(2,1)S(1)} %get-tuple-element.31.refs_1_, ...), custom_call_target="tpu_custom_call" | custom-call | tf_op jit(solution)/shard_map/gather/pallas_call | solution.py:535
  235.0 9.8 %write.1 = (bf16[2,4,4,56,2560]{4,3,2,1,0:T(8,128)(2,1)}, bf16[2,4,4,56,2560]{4,3,2,1,0:T(8,128)(2,1)}, bf16[2,4,4,4,40,896]{5,4,3,2,1,0:T(8,128)(2,1)}, f32[14,...) custom-call(bf16[2,4,4,56,2560]{4,3,2,1,0:T(8,128)(2,1)S(1)} %get-tu, ...), custom_call_target="tpu_custom_call" | custom-call | tf_op jit(solution)/shard_map/write/pallas_call | solution.py:545

commit v2 on v0

v2 whole, which is shorter than its diff:
```python
import functools

import jax
import jax.numpy as jnp
from jax import lax
from jax.experimental import pallas as pl
from jax.experimental.pallas import tpu as pltpu
from jax.sharding import PartitionSpec as P

MESH = pl.DeviceIdType.MESH
F32, BF16 = jnp.float32, jnp.bfloat16
ROWS, PAD = 14, 16
BLOCK, TALL = 4 * ROWS, 40
STRIDE = (16, 4, 1)
X, Y, Z = GATE, UP, DOWN = range(3)
PAIR = (0, 1)
SIGN = (1, -1)
ALL = slice(None)
MIB = 1024 * 1024
STEP_MIB = 34


def place():
    me = lax.axis_index("dp")
    c = (lax.div(me, 16), lax.rem(lax.div(me, 4), 4), lax.rem(me, 4))

    def peer(axis, shift):
        return me + (lax.rem(c[axis] + (shift % 4), 4) - c[axis]) * STRIDE[axis]

    return c, peer


def mod4(value):
    return lax.rem(value + 8, 4)


def greet(peers):
    barrier = pltpu.get_barrier_semaphore()
    for p in peers:
        pl.semaphore_signal(barrier, inc=1, device_id={"dp": p}, device_id_type=MESH)
    pl.semaphore_wait(barrier, len(peers))


class Copies:
    def __init__(self, send, recv):
        self.send, self.recv, self.next, self.made = send, recv, 0, []

    def start(self, src, dst, device):
        n = self.next
        self.next += 1
        copy = pltpu.make_async_remote_copy(
            src_ref=src, dst_ref=dst, send_sem=self.send.at[n], recv_sem=self.recv.at[n],
            device_id={"dp": device}, device_id_type=MESH,
        )
        copy.start()
        self.made.append(copy)
        return copy

    def drain(self):
        for copy in self.made:
            copy.wait_send()
        self.made = []


class Local:
    def __init__(self, sem):
        self.sem, self.next = sem, 0

    def start(self, src, dst):
        copy = pltpu.make_async_copy(src, dst, self.sem.at[self.next])
        self.next += 1
        copy.start()
        return copy


class Ring:
    def __init__(self, copies, c, peer, axis, slot):
        self.copies, self.peer, self.axis, self.slot = copies, peer, axis, slot
        self.k = c[axis]
        self.left, self.right = mod4(self.k - 1), mod4(self.k + 1)
        self.arrive, self.onward = {}, {}

    def start(self, layer):
        here = self.slot(layer, self.k)
        for side in SIGN:
            self.arrive[layer, side] = self.copies.start(here, here, self.peer(self.axis, side))

    def forward(self):
        for layer, k in zip(PAIR, (self.left, self.right)):
            side = SIGN[layer]
            self.arrive[layer, side].wait_recv()
            here = self.slot(layer, k)
            self.onward[layer] = self.copies.start(here, here, self.peer(self.axis, side))

    def near(self):
        for layer in PAIR:
            self.arrive[layer, -SIGN[layer]].wait_recv()

    def far(self):
        for layer in PAIR:
            self.onward[layer].wait_recv()


def step_kernel(cols, count, *refs):
    it = iter(refs)
    take = lambda n: [next(it) for _ in range(n)]
    three = lambda: take(3)
    quarter = cols // 4
    g, w, m, v = three(), three(), three(), three()
    out, new_m, new_v = three(), three(), three()
    sb2, sf2, ro2, rd2, rs2 = three(), three(), three(), three(), three()
    sb3, sf3, ro3, rd3, rs3 = three(), three(), three(), three(), three()
    own_m, own_v, own_w, own_g = three(), three(), three(), three()
    packed = take(2)
    fold, packs, raw_w, raw_m, raw_v, part, parts, send, recv, lsem = take(10)
    (x, y, z), peer = place()
    c = (x, y, z)
    copies, local = Copies(send, recv), Local(lsem)
    AXES = ((X, Y, Z), (Y, Z, X), (Z, X, Y))
    ro1, rd1, rs1, own1 = ([lambda layer, p, a=a, n=n: out[a].at[layer, n, p] for a in range(3)] for n in range(4))
    cases = [(a, layer) for a in range(3) for layer in PAIR]

    def order(axis, layer):
        s = SIGN[layer]
        return [mod4(c[axis] + d) for d in (2, -s, s, 0)]

    def unit(a, layer, k, p):
        if a == GATE:
            return g[a].at[layer, k, order(Y, layer)[p]]
        if a == UP:
            return g[a].at[layer, order(X, layer)[p], k]
        return g[a].at[layer, order(X, layer)[p], :, k]

    small = [local.start(src[a], dst) for src, dsts in ((m, (raw_m.at[GATE], raw_m.at[UP], own_m[DOWN])), (v, (raw_v.at[GATE], raw_v.at[UP], own_v[DOWN]))) for a, dst in enumerate(dsts)]
    small += [local.start(w[a].at[:, x, y], raw_w.at[a]) for a in (GATE, UP)]
    small += [local.start(w[DOWN].at[:, x, y, z], own_w[DOWN])]

    greet([peer(axis, shift) for axis in (X, Y, Z) for shift in (1, 2, 3)])

    opp1, dir1, sum1, mine = {}, {}, {}, {}
    for p in range(4):
        for a, layer in cases:
            ax, s = AXES[a][0], SIGN[layer]
            opp1[a, layer, p] = copies.start(unit(a, layer, mod4(c[ax] + 2), p), ro1[a](layer, p), peer(ax, s))
            mine[a, layer, p] = local.start(unit(a, layer, mod4(c[ax] + s), p), own1[a](layer, p))
    for p in range(4):
        for a, layer in cases:
            ax, s = AXES[a][0], SIGN[layer]
            dir1[a, layer, p] = copies.start(unit(a, layer, mod4(c[ax] - s), p), rd1[a](layer, p), peer(ax, -s))

    def pack(rows):
        for n in range(4):
            fold[0:BLOCK, :] = rows(slice(n * quarter, (n + 1) * quarter))
            for k in range(4):
                packs[k, n * ROWS : n * ROWS + PAD, :] = fold[k * ROWS : k * ROWS + PAD, :]

    def unpack(pieces, dst):
        for k in range(4):
            packs[k, 0:BLOCK, :] = pieces[k].astype(F32)
        for n in range(4):
            for k in range(4):
                fold[k * ROWS : k * ROWS + PAD, :] = packs[k, n * ROWS : n * ROWS + PAD, :]
            dst[:, n * quarter : (n + 1) * quarter] = fold[0:BLOCK, :].astype(BF16)

    fold[BLOCK:, :] = jnp.zeros((64 - BLOCK, quarter), F32)
    packs[:, BLOCK:, :] = jnp.zeros((4, 64 - BLOCK, quarter), F32)
    for copy in small:
        copy.wait()
    for src, dst in ((raw_m, own_m), (raw_v, own_v)):
        for a in (GATE, UP):
            @pl.loop(0, ROWS)
            def _(r):
                rows = src[a, r]
                for layer in PAIR:
                    for n in range(4):
                        dst[a][layer, pl.ds(n * ROWS + r, 1), :] = rows[layer : layer + 1, n * quarter : (n + 1) * quarter]
    for a in (GATE, UP):
        for layer in PAIR:
            pack(lambda at: raw_w[a, layer, :, at].astype(F32))
            own_w[a][layer] = packs[z, 0:BLOCK, :]

    def add(dst, one, two):
        if one.shape[0] == 4:
            for k in range(4):
                dst[k] = (one[k].astype(F32) + two[k].astype(F32)).astype(BF16)
        elif one.shape[1] == cols:
            @pl.loop(0, 4)
            def _(n):
                at = pl.ds(pl.multiple_of(n * quarter, quarter), quarter)
                dst[:, at] = (one[:, at].astype(F32) + two[:, at].astype(F32)).astype(BF16)
        else:
            dst[...] = (one[...].astype(F32) + two[...].astype(F32)).astype(BF16)

    def total(refs, at):
        one, two, three = (r[at].astype(F32) for r in refs)
        return one + two + three

    for p in range(4):
        for a, layer in cases:
            ax, s = AXES[a][0], SIGN[layer]
            opp1[a, layer, p].wait_recv()
            mine[a, layer, p].wait()
            here = ro1[a](layer, p)
            add(here, here, own1[a](layer, p))
            sum1[a, layer, p] = copies.start(here, rs1[a](layer, p), peer(ax, s))
            mine[a, layer, p] = local.start(unit(a, layer, c[ax], p), own1[a](layer, p))

    opp2, dir2, sum2 = {}, {}, {}

    def keep2(a, layer, r2, r3, value):
        ax, s = AXES[a][1], SIGN[layer]
        if r2 >= 2:
            sf2[a][layer, r2 - 2, r3] = value
            return
        sb2[a][layer, r2, r3] = value.astype(BF16)
        here = sb2[a].at[layer, r2, r3]
        if r2 == 0:
            opp2[a, layer, r3] = copies.start(here, ro2[a].at[layer, r3], peer(ax, s))
        else:
            dir2[a, layer, r3] = copies.start(here, rd2[a].at[layer, r3], peer(ax, -s))

    for p in range(4):
        for a, layer in cases:
            sum1[a, layer, p].wait_recv()
            dir1[a, layer, p].wait_recv()
            mine[a, layer, p].wait()
            terms = [b[a](layer, p) for b in (own1, rs1, rd1)]
            pieces = order(Y if a == DOWN else Z, layer)
            if a == DOWN:
                for q, k in enumerate(pieces):
                    keep2(a, layer, p, q, total(terms, k))
                continue
            pack(lambda at: total(terms, (ALL, at)))
            for q, k in enumerate(pieces):
                r2, r3 = (q, p) if a == UP else (p, q)
                keep2(a, layer, r2, r3, packs[k, 0:BLOCK, :])

    for r3 in range(4):
        for a, layer in cases:
            opp2[a, layer, r3].wait_recv()
            here = ro2[a].at[layer, r3]
            add(here, here, sf2[a].at[layer, 0, r3])
            sum2[a, layer, r3] = copies.start(here, rs2[a].at[layer, r3], peer(AXES[a][1], SIGN[layer]))
    copies.drain()

    opp3, dir3, sum3 = {}, {}, {}
    for r3 in range(4):
        for a, layer in cases:
            ax, s = AXES[a][2], SIGN[layer]
            sum2[a, layer, r3].wait_recv()
            dir2[a, layer, r3].wait_recv()
            value = total((sf2[a].at[layer, 1, r3], rs2[a].at[layer, r3], rd2[a].at[layer, r3]), ...)
            if r3 >= 2:
                sf3[a][layer, r3 - 2] = value
                continue
            sb3[a][layer, r3] = value.astype(BF16)
            here = sb3[a].at[layer, r3]
            if r3 == 0:
                opp3[a, layer] = copies.start(here, ro3[a].at[layer], peer(ax, s))
            else:
                dir3[a, layer] = copies.start(here, rd3[a].at[layer], peer(ax, -s))
        if r3 == 2:
            for a, layer in cases:
                opp3[a, layer].wait_recv()
                here = ro3[a].at[layer]
                add(here, here, sf3[a].at[layer, 0])
                sum3[a, layer] = copies.start(here, rs3[a].at[layer], peer(AXES[a][2], SIGN[layer]))

    part[...] = jnp.zeros((8, 128), F32)
    for a, layer in cases:
        sum3[a, layer].wait_recv()
        dir3[a, layer].wait_recv()
        value = total((sf3[a].at[layer, 1], rs3[a].at[layer], rd3[a].at[layer]), ...)
        value = value.astype(BF16).astype(F32)
        own_g[a][layer] = value
        value = value * value
        lines = sum(value[r : r + 8] for r in range(0, value.shape[0], 8))
        part[...] += sum(lines[:, k : k + 128] for k in range(0, value.shape[1], 128))

    value = part[...]
    for axis in (X, Y, Z):
        own = parts.at[axis, c[axis]]
        own[...] = value
        line = [copies.start(own, own, peer(axis, shift)) for shift in (1, 2, 3)]
        for copy in line:
            copy.wait_recv()
        value = (parts[axis, 0] + parts[axis, 1]) + (parts[axis, 2] + parts[axis, 3])
    squares = jnp.full((8, 128), jnp.sum(value), F32)
    factor = jnp.minimum(1.0, 0.5 * lax.rsqrt(squares / count + 1e-30))[0:1, 0:1]

    ring = functools.partial(Ring, copies, c, peer)

    def piece(a, i, j):
        if a == DOWN:
            return lambda layer: out[a].at[layer, i, j, z]
        return lambda layer: packed[a].at[layer, i, j]

    def slot1(a):
        if a == UP:
            return lambda layer, k: piece(a, k, z)(layer)
        return lambda layer, k: piece(a, y if a == GATE else x, k)(layer)

    def slot2(a, fixed):
        if a == UP:
            return lambda layer, k: piece(a, fixed, k)(layer)
        return lambda layer, k: piece(a, k, fixed)(layer)

    def slot3(a, fixed):
        if a == GATE:
            return lambda layer, k: out[a].at[layer, k, fixed]
        if a == UP:
            return lambda layer, k: out[a].at[layer, fixed, k]
        return lambda layer, k: out[a].at[layer, fixed, :, k]

    def near_first(axis):
        return [mod4(c[axis] + d) for d in (0, -1, 1, 2)]

    first = [ring(AXES[a][2], slot1(a)) for a in range(3)]
    second = [[ring(AXES[a][1], slot2(a, k)) for k in near_first(AXES[a][2])] for a in range(3)]
    BLOCKS = (Y, X, X)
    third = [[ring(AXES[a][0], slot3(a, k)) for k in near_first(BLOCKS[a])] for a in range(3)]

    for a, layer in cases:
        gg = own_g[a][layer] * factor
        ww = own_w[a][layer].astype(F32)
        mm = 0.9 * own_m[a][layer] + 0.1 * gg
        vv = 0.95 * own_v[a][layer] + 0.05 * gg * gg
        new_m[a][layer], new_v[a][layer] = mm, vv
        here = first[a].slot(layer, c[AXES[a][2]])
        here[...] = (ww - 0.02 * (mm * lax.rsqrt(vv + 1e-8) + 0.1 * ww)).astype(BF16)
        first[a].start(layer)
        second[a][0].start(layer)

    def last(a, n):
        k = near_first(BLOCKS[a])[n]
        for layer in PAIR:
            if a != DOWN:
                unpack(packed[a].at[layer, k], third[a][n].slot(layer, c[AXES[a][0]]))
            third[a][n].start(layer)

    for r in first:
        r.forward()
    for a in range(3):
        first[a].near()
        for r in second[a][1:3]:
            for layer in PAIR:
                r.start(layer)
    for a in range(3):
        first[a].far()
        for layer in PAIR:
            second[a][3].start(layer)
    last(DOWN, 0)
    last(GATE, 0)
    for n in range(4):
        for a in range(3):
            second[a][n].forward()
        if n == 1:
            second[UP][0].near()
            second[UP][0].far()
            last(UP, 0)
    for a in (DOWN, GATE):
        for r in second[a]:
            r.near()
        last(a, 1)
        last(a, 2)
    for n in range(1, 4):
        second[UP][n].near()
        second[UP][n].far()
        last(UP, n)
    for a in (DOWN, GATE):
        for r in second[a]:
            r.far()
        last(a, 3)
    for n in range(4):
        for a in range(3):
            third[a][n].forward()
    for n in range(4):
        for a in range(3):
            third[a][n].near()
            third[a][n].far()
    copies.drain()


def write_kernel(*refs):
    it = iter(refs)
    take = lambda n: [next(it) for _ in range(n)]
    three = lambda: take(3)
    w, m, v = three(), three(), three()
    out_w, out_m, out_v = three(), three(), three()
    pairs, sem = take(2)
    quarter = m[GATE].shape[-1]
    local = Local(sem)
    copies = [local.start(w[a].at[layer, k], out_w[a].at[layer, k]) for a in range(3) for layer in PAIR for k in range(4)]
    copies += [local.start(m[DOWN], out_m[DOWN]), local.start(v[DOWN], out_v[DOWN])]
    for i, (src, dst) in enumerate((s[a], d[a]) for s, d in ((m, out_m), (v, out_v)) for a in (GATE, UP)):
        @pl.loop(0, ROWS)
        def _(r):
            for layer in PAIR:
                for n in range(4):
                    pairs[i, r, layer : layer + 1, n * quarter : (n + 1) * quarter] = src[layer, pl.ds(n * ROWS + r, 1), :]
        copies.append(local.start(pairs.at[i], dst))
    for copy in copies:
        copy.wait()


def solution(mesh):
    def step(*arrays):
        terms, weights, m, v = (arrays[i : i + 3] for i in (0, 3, 6, 9))
        cols, fcols = terms[GATE].shape[-1], terms[DOWN].shape[-1]
        rows, frows = terms[GATE].shape[-2], terms[DOWN].shape[-2]
        assert rows == 64 * ROWS and frows == 64 * TALL and cols % 512 == 0
        wide = lambda t: t.reshape(2, 4, 4, BLOCK, cols)
        tall = lambda t: t.reshape(2, 4, 4, 4, TALL, fcols)
        shaped = lambda three: (*map(wide, three[:DOWN]), tall(three[DOWN]))
        turn = lambda t: t.transpose(1, 0, 2)
        turned = lambda three: (*map(turn, three[:DOWN]), three[DOWN])
        count = 2 * (2 * rows * cols + frows * fcols)
        anywhere, on_chip = pl.BlockSpec(memory_space=pl.ANY), pl.BlockSpec(memory_space=pltpu.VMEM)
        piece = (BLOCK, cols // 4)
        pieces = (piece, piece, (TALL, fcols))
        every = lambda dtype, *lead: [pltpu.VMEM((*lead, *p), dtype) for p in pieces]
        scratch = [*every(BF16, 2, 2, 4), *every(F32, 2, 2, 4), *every(BF16, 2, 4), *every(BF16, 2, 4), *every(BF16, 2, 4)]
        scratch += [*every(BF16, 2, 2), *every(F32, 2, 2), *every(BF16, 2), *every(BF16, 2), *every(BF16, 2)]
        scratch += [*every(F32, 2), *every(F32, 2), *every(F32, 2)[:DOWN], every(BF16, 2)[DOWN], *every(F32, 2)]
        scratch += every(BF16, 2, 4, 4)[:DOWN]
        scratch += [pltpu.VMEM((64, cols // 4), F32), pltpu.VMEM((4, 64, cols // 4), F32), pltpu.VMEM((2, 2, BLOCK, cols), BF16)]
        scratch += [pltpu.VMEM((2, ROWS, 2, cols), F32)] * 2
        scratch += [pltpu.VMEM((8, 128), F32), pltpu.VMEM((3, 4, 8, 128), F32)]
        scratch += [pltpu.SemaphoreType.DMA((n,)) for n in (333, 333, 57)]
        big = [(2, 4, 4, BLOCK, cols), (2, 4, 4, BLOCK, cols), (2, 4, 4, 4, TALL, fcols)]
        made = pl.pallas_call(
            functools.partial(step_kernel, cols, count),
            out_shape=[pltpu.VMEM(s, BF16) for s in big] + [pltpu.VMEM((2, *p), F32) for p in pieces * 2],
            in_specs=[anywhere] * 12,
            out_specs=[on_chip] * 9,
            scratch_shapes=scratch,
            compiler_params=pltpu.CompilerParams(collective_id=0, has_side_effects=True, vmem_limit_bytes=STEP_MIB * MIB),
            name="step",
        )(*shaped([t[0] for t in terms]), *shaped(weights), *turned(m), *turned(v))
        ends = [(ROWS, 2, cols), (ROWS, 2, cols), (2, TALL, fcols)]
        outs = pl.pallas_call(
            write_kernel,
            out_shape=[jax.ShapeDtypeStruct(s, BF16) for s in big] + [jax.ShapeDtypeStruct(s, F32) for s in ends * 2],
            in_specs=[on_chip] * 9,
            out_specs=[anywhere] * 9,
            scratch_shapes=[pltpu.VMEM((4, ROWS, 2, cols), F32), pltpu.SemaphoreType.DMA((30,))],
            compiler_params=pltpu.CompilerParams(vmem_limit_bytes=16 * MIB),
            name="write",
        )(*made)
        news = tuple(one.reshape(w.shape) for one, w in zip(outs, weights))
        return (*news, *turned(outs[3:6]), *turned(outs[6:9]))

    all_of, cut = P(None, None, None), P(None, "dp", None)
    return jax.shard_map(
        step,
        mesh=mesh,
        in_specs=(P(("rep", "dp"), None, None, None),) * 3 + (all_of,) * 3 + (cut,) * 6,
        out_specs=(P("rep", None, None),) * 3 + (P("rep", "dp", None),) * 6,
        check_vma=False,
    )
```

time: 1110 us -> 253 us (0.23)
  waiting for transfers between devices: 765 us -> 0 us
  Pallas kernels: 0 us -> 238 us
  blocking collectives: 173 us -> 0 us
  local copies, waits for them, and re-layouts: 144 us -> 14.5 us
  between operations: 17.2 us -> 0.67 us
    unnamed x7 -> x0, waiting for transfers between devices: 545 us -> none
    pallas_call x0 -> x2, Pallas kernels: none -> 238 us  [the longest x1 228 us: step(): pl.pallas_call(functools.partial(step_kernel, cols, count), out_shape=[pl...]
    all_gather x3 -> x0, waiting for transfers between devices: 220 us -> none  [step(): whole = [lax.all_gather(one[0], 'dp', axis=1, tiled=True) for one in new]]
    psum x1 -> x0, blocking collectives: 173 us -> none  [step(): squares = lax.psum(sum((jnp.sum(g * g) for g in gradients)), 'dp')]
    unnamed x25 -> x8, local copies, waits for them, and re-layouts: 142 us -> 14.5 us
  transfers between devices with their start and end apart: 5 -> 0, of which waited for: 5 -> 0; matrix products, arithmetic and copies ran while one was open for 7% -> 0% of each run, Pallas kernels for 0% -> 0%
where the time goes in v2:
time: 253 us
  Pallas kernels  238 us (94%)
  local copies, waits for them, and re-layouts  14.5 us (6%)
    pallas_call x1, Pallas kernels, step(): pl.pallas_call(functools.partial(step_kernel, cols, count), out_shape=[pl...  228 us
    unnamed x8, local copies, waits for them, and re-layouts  14.5 us
    pallas_call x1, Pallas kernels, step(): pl.pallas_call(write_kernel, out_shape=[jax.ShapeDtypeStruct(s, BF16) for...  9.81 us

profile of v2, /device:TPU:0, one launch (start us, length us, event | category | flops | bytes accessed | tf_op | source)
XLA Modules:
  0.0 253.0 jit_solution(2097124124694608593)
XLA Ops:
  0.6 228.0 %step.1 = (bf16[2,4,4,56,2560]{4,3,2,1,0:T(8,128)(2,1)S(1)}, bf16[2,4,4,56,2560]{4,3,2,1,0:T(8,128)(2,1)S(1)}, bf16[2,4,4,4,40,896]{5,4,3,2,1,0:T(8,128)(2,1)S(1...) custom-call(bf16[2,4,4,56,2560]{4,3,2,1,0:T(8,128)(2,1)} %bitcast.17, ...), custom_call_target="tpu_custom_call" | custom-call | tf_op jit(solution)/shard_map/step/pallas_call | solution.py:431
  228.7 0.0 copy-start
  228.7 3.6 %copy-done = bf16[2,4,4,56,2560]{4,3,2,1,0:T(8,128)(2,1)} copy-done((bf16[2,4,4,56,2560]{4,3,2,1,0:T(8,128)(2,1)}, bf16[2,4,4,56,2560]{4,3,2,1,0:T(8,128)(2,1)S(1)}, u32[]{:S(2)}) %copy-start) | copy-done | bytes 9175064
  232.4 0.0 copy-start.2
  232.4 3.7 %copy-done.2 = bf16[2,4,4,56,2560]{4,3,2,1,0:T(8,128)(2,1)} copy-done((bf16[2,4,4,56,2560]{4,3,2,1,0:T(8,128)(2,1)}, bf16[2,4,4,56,2560]{4,3,2,1,0:T(8,128)(2,1)S(1)}, u32[]{:S(2)}) %copy-start.2) | copy-done | bytes 9175064
  236.0 0.0 copy-start.1
  236.0 3.6 %copy-done.1 = bf16[2,4,4,56,2560]{4,3,2,1,0:T(8,128)(2,1)S(1)} copy-done((bf16[2,4,4,56,2560]{4,3,2,1,0:T(8,128)(2,1)S(1)}, bf16[2,4,4,56,2560]{4,3,2,1,0:T(8,128)(2,1)}, u32[]{:S(2)}) %copy-start.1) | copy-done | bytes 9175064
  239.6 0.0 copy-start.3
  239.6 3.6 %copy-done.3 = bf16[2,4,4,56,2560]{4,3,2,1,0:T(8,128)(2,1)S(1)} copy-done((bf16[2,4,4,56,2560]{4,3,2,1,0:T(8,128)(2,1)S(1)}, bf16[2,4,4,56,2560]{4,3,2,1,0:T(8,128)(2,1)}, u32[]{:S(2)}) %copy-start.3) | copy-done | bytes 9175064
  243.2 9.8 %write.1 = (bf16[2,4,4,56,2560]{4,3,2,1,0:T(8,128)(2,1)}, bf16[2,4,4,56,2560]{4,3,2,1,0:T(8,128)(2,1)}, bf16[2,4,4,4,40,896]{5,4,3,2,1,0:T(8,128)(2,1)}, f32[14,...) custom-call(bf16[2,4,4,56,2560]{4,3,2,1,0:T(8,128)(2,1)S(1)} %copy-d, ...), custom_call_target="tpu_custom_call" | custom-call | tf_op jit(solution)/shard_map/write/pallas_call | solution.py:441
Async XLA Ops:
  228.7 3.7 %copy-start = (bf16[2,4,4,56,2560]{4,3,2,1,0:T(8,128)(2,1)}, bf16[2,4,4,56,2560]{4,3,2,1,0:T(8,128)(2,1)S(1)}, u32[]{:S(2)}) copy-start(bf16[2,4,4,56,2560]{4,3,2,1,0:T(8,128)(2,1)S(1)} %get-tuple-element.27.refs_0_) | copy-start | bytes 27525124
  232.4 3.7 %copy-start.2 = (bf16[2,4,4,56,2560]{4,3,2,1,0:T(8,128)(2,1)}, bf16[2,4,4,56,2560]{4,3,2,1,0:T(8,128)(2,1)S(1)}, u32[]{:S(2)}) copy-start(bf16[2,4,4,56,2560]{4,3,2,1,0:T(8,128)(2,1)S(1)} %get-tuple-element.28.refs_1_) | copy-start | bytes 27525124
  236.0 3.6 %copy-start.1 = (bf16[2,4,4,56,2560]{4,3,2,1,0:T(8,128)(2,1)S(1)}, bf16[2,4,4,56,2560]{4,3,2,1,0:T(8,128)(2,1)}, u32[]{:S(2)}) copy-start(bf16[2,4,4,56,2560]{4,3,2,1,0:T(8,128)(2,1)} %copy-done) | copy-start | bytes 27525124
  239.6 3.6 %copy-start.3 = (bf16[2,4,4,56,2560]{4,3,2,1,0:T(8,128)(2,1)S(1)}, bf16[2,4,4,56,2560]{4,3,2,1,0:T(8,128)(2,1)}, u32[]{:S(2)}) copy-start(bf16[2,4,4,56,2560]{4,3,2,1,0:T(8,128)(2,1)} %copy-done.2) | copy-start | bytes 27525124

commit v3 on v2

--- a/solution.py
+++ b/solution.py
@@ -414,8 +414,9 @@
         shaped = lambda three: (*map(wide, three[:DOWN]), tall(three[DOWN]))
         turn = lambda t: t.transpose(1, 0, 2)
         turned = lambda three: (*map(turn, three[:DOWN]), three[DOWN])
+        stay = lambda t: pltpu.with_memory_space_constraint(t, pltpu.HBM)
         count = 2 * (2 * rows * cols + frows * fcols)
-        anywhere, on_chip = pl.BlockSpec(memory_space=pl.ANY), pl.BlockSpec(memory_space=pltpu.VMEM)
+        anywhere, on_chip, off_chip = (pl.BlockSpec(memory_space=space) for space in (pl.ANY, pltpu.VMEM, pltpu.HBM))
         piece = (BLOCK, cols // 4)
         pieces = (piece, piece, (TALL, fcols))
         every = lambda dtype, *lead: [pltpu.VMEM((*lead, *p), dtype) for p in pieces]
@@ -431,12 +432,12 @@
         made = pl.pallas_call(
             functools.partial(step_kernel, cols, count),
             out_shape=[pltpu.VMEM(s, BF16) for s in big] + [pltpu.VMEM((2, *p), F32) for p in pieces * 2],
-            in_specs=[anywhere] * 12,
+            in_specs=[off_chip] * 12,
             out_specs=[on_chip] * 9,
             scratch_shapes=scratch,
             compiler_params=pltpu.CompilerParams(collective_id=0, has_side_effects=True, vmem_limit_bytes=STEP_MIB * MIB),
             name="step",
-        )(*shaped([t[0] for t in terms]), *shaped(weights), *turned(m), *turned(v))
+        )(*shaped([t[0] for t in terms]), *shaped(weights), *map(stay, (*turned(m), *turned(v))))
         ends = [(ROWS, 2, cols), (ROWS, 2, cols), (2, TALL, fcols)]
         outs = pl.pallas_call(
             write_kernel,
@@ -444,7 +445,7 @@
             in_specs=[on_chip] * 9,
             out_specs=[anywhere] * 9,
             scratch_shapes=[pltpu.VMEM((4, ROWS, 2, cols), F32), pltpu.SemaphoreType.DMA((30,))],
-            compiler_params=pltpu.CompilerParams(vmem_limit_bytes=16 * MIB),
+            compiler_params=pltpu.CompilerParams(vmem_limit_bytes=2 * MIB),
             name="write",
         )(*made)
         news = tuple(one.reshape(w.shape) for one, w in zip(outs, weights))

time: 253 us -> 239 us (0.945)
  local copies, waits for them, and re-layouts: 14.5 us -> 0 us
    unnamed x8 -> x0, local copies, waits for them, and re-layouts: 14.5 us -> none
where the time goes in v3:
time: 239 us
  Pallas kernels  238 us (100%)
    pallas_call x1, Pallas kernels, step(): pl.pallas_call(functools.partial(step_kernel, cols, count), out_shape=[pl...  228 us
    pallas_call x1, Pallas kernels, step(): pl.pallas_call(write_kernel, out_shape=[jax.ShapeDtypeStruct(s, BF16) for...  9.82 us

profile of v3, /device:TPU:0, one launch (start us, length us, event | category | flops | bytes accessed | tf_op | source)
XLA Modules:
  0.0 238.5 jit_solution(6890478672791550881)
XLA Ops:
  0.6 228.0 %step.1 = (bf16[2,4,4,56,2560]{4,3,2,1,0:T(8,128)(2,1)S(1)}, bf16[2,4,4,56,2560]{4,3,2,1,0:T(8,128)(2,1)S(1)}, bf16[2,4,4,4,40,896]{5,4,3,2,1,0:T(8,128)(2,1)S(1...) custom-call(bf16[2,4,4,56,2560]{4,3,2,1,0:T(8,128)(2,1)} %bitcast.17, ...), custom_call_target="tpu_custom_call" | custom-call | tf_op jit(solution)/shard_map/step/pallas_call | solution.py:432
  228.7 9.8 %write.1 = (bf16[2,4,4,56,2560]{4,3,2,1,0:T(8,128)(2,1)}, bf16[2,4,4,56,2560]{4,3,2,1,0:T(8,128)(2,1)}, bf16[2,4,4,4,40,896]{5,4,3,2,1,0:T(8,128)(2,1)}, f32[14,...) custom-call(bf16[2,4,4,56,2560]{4,3,2,1,0:T(8,128)(2,1)S(1)} %get-tu, ...), custom_call_target="tpu_custom_call" | custom-call | tf_op jit(solution)/shard_map/write/pallas_call | solution.py:442

commit v4 on v3

v4 whole, which is shorter than its diff:
```python
import functools

import jax
import jax.numpy as jnp
from jax import lax
from jax.experimental import pallas as pl
from jax.experimental.pallas import tpu as pltpu
from jax.sharding import PartitionSpec as P

MESH = pl.DeviceIdType.MESH
F32, BF16 = jnp.float32, jnp.bfloat16
ROWS, PAD = 14, 16
BLOCK, TALL = 4 * ROWS, 40
STRIDE = (16, 4, 1)
X, Y, Z = GATE, UP, DOWN = range(3)
PAIR = (0, 1)
SIGN = (1, -1)
ALL = slice(None)
MIB = 1024 * 1024
STEP_MIB = 34


def place():
    me = lax.axis_index("dp")
    c = (lax.div(me, 16), lax.rem(lax.div(me, 4), 4), lax.rem(me, 4))

    def peer(axis, shift):
        return me + (lax.rem(c[axis] + (shift % 4), 4) - c[axis]) * STRIDE[axis]

    return c, peer


def mod4(value):
    return lax.rem(value + 8, 4)


def greet(peers):
    barrier = pltpu.get_barrier_semaphore()
    for p in peers:
        pl.semaphore_signal(barrier, inc=1, device_id={"dp": p}, device_id_type=MESH)
    pl.semaphore_wait(barrier, len(peers))


class Sends:
    def __init__(self, send, recv):
        self.send, self.recv, self.next = send, recv, 0

    def semaphore(self):
        self.next += 1
        return self.recv.at[self.next - 1]

    def start(self, group, src, dst, device, arrival):
        pltpu.make_async_remote_copy(
            src_ref=src, dst_ref=dst, send_sem=self.send.at[group], recv_sem=arrival, device_id={"dp": device}, device_id_type=MESH
        ).start()


def await_bytes(ref, semaphore):
    pltpu.make_async_copy(ref, ref, semaphore).wait()


class Ring:
    def __init__(self, sends, c, peer, group, axis, slot, onward, near, far):
        self.sends, self.peer, self.group, self.axis, self.slot = sends, peer, group, axis, slot
        self.k = c[axis]
        self.left, self.right = mod4(self.k - 1), mod4(self.k + 1)
        self.onward, self.near, self.far = onward, near, far

    def start(self, layer):
        here = self.slot(layer, self.k)
        self.sends.start(self.group, here, here, self.peer(self.axis, SIGN[layer]), self.onward)
        self.sends.start(self.group, here, here, self.peer(self.axis, -SIGN[layer]), self.near)

    def forward(self):
        await_bytes(self.slot(ALL, self.left), self.onward)
        for layer, k in zip(PAIR, (self.left, self.right)):
            here = self.slot(layer, k)
            self.sends.start(self.group, here, here, self.peer(self.axis, SIGN[layer]), self.far)


def step_kernel(cols, count, *refs):
    it = iter(refs)
    take = lambda n: [next(it) for _ in range(n)]
    three = lambda: take(3)
    quarter = cols // 4
    g, w, m, v = three(), three(), three(), three()
    out, new_m, new_v = three(), three(), three()
    sb2, sf2, ro2, rx2 = three(), three(), three(), three()
    sb3, sf3, ro3, rx3 = three(), three(), three(), three()
    own_m, own_v, own_w, own_g = three(), three(), three(), three()
    packed = take(2)
    fold, packs, raw_w, raw_m, raw_v, parts, send, recv, lsem, psem = take(10)
    (x, y, z), peer = place()
    c = (x, y, z)
    sends = Sends(send, recv)
    AXES = ((X, Y, Z), (Y, Z, X), (Z, X, Y))
    ro1, rd1, rs1, own1 = ([lambda layer, p, a=a, n=n: out[a].at[layer, n, p] for a in range(3)] for n in range(4))
    cases = [(a, p) for p in range(4) for a in range(3)]

    def order(axis, layer):
        s = SIGN[layer]
        return [mod4(c[axis] + d) for d in (2, -s, s, 0)]

    def block(a, layer, k, j):
        if a == GATE:
            return g[a].at[layer, k, j]
        if a == UP:
            return g[a].at[layer, j, k]
        return g[a].at[layer, j, :, k]

    UNITS = (Y, X, X)

    def unit(a, layer, k, p):
        return block(a, layer, k, order(UNITS[a], layer)[p])

    def mine(a, layer, role):
        k = order(AXES[a][0], layer)[role]
        return pltpu.make_async_copy(block(a, layer, k, ALL), out[a].at[layer, 3], lsem.at[2 * a + layer])

    def sent(a, phase):
        if phase == 0:
            ref = out[a].at[:, 0:3]
        elif phase == 1:
            ref = out[a].at[:, 0:3, :, 0] if a == DOWN else packed[a].at[:, 0:3]
        else:
            ref = out[a].at[:, 0:3, 0, 0] if a == DOWN else packed[a].at[:, 0:3, 0]
        await_bytes(ref, send.at[3 * phase + a])

    greet([peer(axis, side) for axis in (X, Y, Z) for side in SIGN])

    opp1, end1 = ({case: sends.semaphore() for case in cases} for _ in range(2))
    for a, p in cases:
        for layer in PAIR:
            ax, s = AXES[a][0], SIGN[layer]
            sends.start(a, unit(a, layer, mod4(c[ax] + 2), p), ro1[a](layer, p), peer(ax, s), opp1[a, p])
            if p == 0:
                mine(a, layer, 2).start()
    for a, p in cases:
        for layer in PAIR:
            ax, s = AXES[a][0], SIGN[layer]
            sends.start(a, unit(a, layer, mod4(c[ax] - s), p), rd1[a](layer, p), peer(ax, -s), end1[a, p])
    small = []
    for n, (src, raw, whole) in enumerate(((m, raw_m, own_m), (v, raw_v, own_v), (w, raw_w, own_w))):
        one, other = lsem.at[6 + n], lsem.at[9 + n]
        for a in (GATE, UP):
            pltpu.make_async_copy(src[a].at[:, x, y] if n == 2 else src[a], raw.at[a], one).start()
        last = pltpu.make_async_copy(src[DOWN].at[:, x, y, z] if n == 2 else src[DOWN], whole[DOWN], other)
        last.start()
        small += [pltpu.make_async_copy(raw, raw, one), last]

    def pack(rows):
        for n in range(4):
            fold[0:BLOCK, :] = rows(slice(n * quarter, (n + 1) * quarter))
            for k in range(4):
                packs[k, n * ROWS : n * ROWS + PAD, :] = fold[k * ROWS : k * ROWS + PAD, :]

    def unpack(pieces, dst):
        for k in range(4):
            packs[k, 0:BLOCK, :] = pieces[k].astype(F32)
        for n in range(4):
            for k in range(4):
                fold[k * ROWS : k * ROWS + PAD, :] = packs[k, n * ROWS : n * ROWS + PAD, :]
            dst[:, n * quarter : (n + 1) * quarter] = fold[0:BLOCK, :].astype(BF16)

    fold[BLOCK:, :] = jnp.zeros((64 - BLOCK, quarter), F32)
    packs[:, BLOCK:, :] = jnp.zeros((4, 64 - BLOCK, quarter), F32)
    for copy in small:
        copy.wait()
    for src, dst in ((raw_m, own_m), (raw_v, own_v)):
        for a in (GATE, UP):
            @pl.loop(0, ROWS)
            def _(r):
                rows = src[a, r]
                for layer in PAIR:
                    for n in range(4):
                        dst[a][layer, pl.ds(n * ROWS + r, 1), :] = rows[layer : layer + 1, n * quarter : (n + 1) * quarter]
    for a in (GATE, UP):
        for layer in PAIR:
            pack(lambda at: raw_w[a, layer, :, at].astype(F32))
            own_w[a][layer] = packs[z, 0:BLOCK, :]

    def add(dst, one, two):
        if one.shape[0] == 4:
            for k in range(4):
                dst[k] = (one[k].astype(F32) + two[k].astype(F32)).astype(BF16)
        elif one.shape[1] == cols:
            @pl.loop(0, 4)
            def _(n):
                at = pl.ds(pl.multiple_of(n * quarter, quarter), quarter)
                dst[:, at] = (one[:, at].astype(F32) + two[:, at].astype(F32)).astype(BF16)
        else:
            dst[...] = (one[...].astype(F32) + two[...].astype(F32)).astype(BF16)

    def total(refs, at):
        one, two, three = (r[at].astype(F32) for r in refs)
        return one + two + three

    for a, p in cases:
        await_bytes(out[a].at[:, 0, p], opp1[a, p])
        for layer in PAIR:
            if p == 0:
                mine(a, layer, 2).wait()
            here = ro1[a](layer, p)
            add(here, here, own1[a](layer, order(UNITS[a], layer)[p]))
            sends.start(a, here, rs1[a](layer, p), peer(AXES[a][0], SIGN[layer]), end1[a, p])
            if p == 3:
                mine(a, layer, 3).start()

    opp2, end2 = ({case: sends.semaphore() for case in cases} for _ in range(2))

    def keep2(a, layer, r2, r3, value):
        ax, s = AXES[a][1], SIGN[layer]
        if r2 >= 2:
            sf2[a][layer, r2 - 2, r3] = value
            return
        sb2[a][layer, r2, r3] = value.astype(BF16)
        here = sb2[a].at[layer, r2, r3]
        if r2 == 0:
            sends.start(3 + a, here, ro2[a].at[layer, r3], peer(ax, s), opp2[a, r3])
        else:
            sends.start(3 + a, here, rx2[a].at[layer, 0, r3], peer(ax, -s), end2[a, r3])

    for a, p in cases:
        await_bytes(out[a].at[:, 1:3, p], end1[a, p])
        for layer in PAIR:
            if p == 0:
                mine(a, layer, 3).wait()
            terms = [own1[a](layer, order(UNITS[a], layer)[p]), rs1[a](layer, p), rd1[a](layer, p)]
            pieces = order(Y if a == DOWN else Z, layer)
            if a == DOWN:
                for q, k in enumerate(pieces):
                    keep2(a, layer, p, q, total(terms, k))
                continue
            pack(lambda at: total(terms, (ALL, at)))
            for q, k in enumerate(pieces):
                r2, r3 = (q, p) if a == UP else (p, q)
                keep2(a, layer, r2, r3, packs[k, 0:BLOCK, :])

    for a, r3 in cases:
        await_bytes(ro2[a].at[:, r3], opp2[a, r3])
        for layer in PAIR:
            here = ro2[a].at[layer, r3]
            add(here, here, sf2[a].at[layer, 0, r3])
            sends.start(3 + a, here, rx2[a].at[layer, 1, r3], peer(AXES[a][1], SIGN[layer]), end2[a, r3])
    for a in range(3):
        sent(a, 0)

    opp3, end3 = ([sends.semaphore() for _ in range(3)] for _ in range(2))
    for a, r3 in cases:
        await_bytes(rx2[a].at[:, :, r3], end2[a, r3])
        for layer in PAIR:
            ax, s = AXES[a][2], SIGN[layer]
            value = total((sf2[a].at[layer, 1, r3], rx2[a].at[layer, 0, r3], rx2[a].at[layer, 1, r3]), ...)
            if r3 >= 2:
                sf3[a][layer, r3 - 2] = value
                continue
            sb3[a][layer, r3] = value.astype(BF16)
            here = sb3[a].at[layer, r3]
            if r3 == 0:
                sends.start(6 + a, here, ro3[a].at[layer], peer(ax, s), opp3[a])
            else:
                sends.start(6 + a, here, rx3[a].at[layer, 0], peer(ax, -s), end3[a])
        if r3 == 2:
            await_bytes(ro3[a], opp3[a])
            for layer in PAIR:
                here = ro3[a].at[layer]
                add(here, here, sf3[a].at[layer, 0])
                sends.start(6 + a, here, rx3[a].at[layer, 1], peer(AXES[a][2], SIGN[layer]), end3[a])

    lines = jnp.zeros((8, 128), F32)
    for a in range(3):
        await_bytes(rx3[a], end3[a])
        for layer in PAIR:
            value = total((sf3[a].at[layer, 1], rx3[a].at[layer, 0], rx3[a].at[layer, 1]), ...)
            value = value.astype(BF16).astype(F32)
            own_g[a][layer] = value
            value = value * value
            value = sum(value[r : r + 8] for r in range(0, value.shape[0], 8))
            lines += sum(value[:, k : k + 128] for k in range(0, value.shape[1], 128))

    me = lax.axis_index("dp")
    parts[me] = jnp.sum(lines, axis=0, keepdims=True)

    @pl.loop(1, 64)
    def _(n):
        pltpu.make_async_remote_copy(
            src_ref=parts.at[me], dst_ref=parts.at[me], send_sem=psem.at[0], recv_sem=psem.at[1],
            device_id={"dp": lax.rem(me + n, 64)}, device_id_type=MESH,
        ).start()
    for a in range(3):
        sent(a, 1)
        sent(a, 2)
    await_bytes(parts.at[0:63], psem.at[1])
    value = jnp.sum(parts[...], axis=0)
    squares = jnp.full((8, 128), jnp.sum(value), F32)
    factor = jnp.minimum(1.0, 0.5 * lax.rsqrt(squares / count + 1e-30))[0:1, 0:1]

    sends.next = 0

    def piece(a, i, j):
        if a == DOWN:
            return lambda layer: out[a].at[layer, i, j, z]
        return lambda layer: packed[a].at[layer, i, j]

    def slot1(a):
        if a == UP:
            return lambda layer, k: piece(a, k, z)(layer)
        return lambda layer, k: piece(a, y if a == GATE else x, k)(layer)

    def slot2(a, fixed):
        if a == UP:
            return lambda layer, k: piece(a, fixed, k)(layer)
        return lambda layer, k: piece(a, k, fixed)(layer)

    def slot3(a, fixed):
        if a == GATE:
            return lambda layer, k: out[a].at[layer, k, fixed]
        if a == UP:
            return lambda layer, k: out[a].at[layer, fixed, k]
        return lambda layer, k: out[a].at[layer, fixed, :, k]

    def near_first(axis):
        return [mod4(c[axis] + d) for d in (0, -1, 1, 2)]

    def rings(a, phase, slot, fixed, shared):
        near, far = (sends.semaphore() for _ in range(2)) if shared else (None, None)
        made = []
        for k in fixed:
            end = None if shared else sends.semaphore()
            made.append(Ring(sends, c, peer, 3 * phase + a, AXES[a][phase], slot(k), sends.semaphore(), near or end, far or end))
        return made

    first = [rings(a, 2, lambda _, a=a: slot1(a), [0], True)[0] for a in range(3)]
    second = [rings(a, 1, functools.partial(slot2, a), near_first(AXES[a][2]), a != UP) for a in range(3)]
    third = [rings(a, 0, functools.partial(slot3, a), near_first(UNITS[a]), False) for a in range(3)]

    for a in range(3):
        for layer in PAIR:
            gg = own_g[a][layer] * factor
            ww = own_w[a][layer].astype(F32)
            mm = 0.9 * own_m[a][layer] + 0.1 * gg
            vv = 0.95 * own_v[a][layer] + 0.05 * gg * gg
            here = first[a].slot(layer, c[AXES[a][2]])
            here[...] = (ww - 0.02 * (mm * lax.rsqrt(vv + 1e-8) + 0.1 * ww)).astype(BF16)
            first[a].start(layer)
            second[a][0].start(layer)
            own_m[a][layer], own_v[a][layer] = mm, vv

    def last(a, n):
        k = near_first(UNITS[a])[n]
        for layer in PAIR:
            if a != DOWN:
                unpack(packed[a].at[layer, k], third[a][n].slot(layer, c[AXES[a][0]]))
            third[a][n].start(layer)

    def near2(a):
        await_bytes(out[a].at[:, 0, :, 0] if a == DOWN else packed[a].at[:, 0], second[a][0].near)

    def far2(a):
        await_bytes(out[a].at[:, 0, :, 0] if a == DOWN else packed[a].at[:, 0], second[a][0].far)

    def up2(n):
        await_bytes(packed[UP].at[:, 0, 0:2], second[UP][n].near)

    for r in first:
        r.forward()
    for a in range(3):
        await_bytes(first[a].slot(ALL, 0), first[a].near)
        for r in second[a][1:3]:
            for layer in PAIR:
                r.start(layer)
    for a in range(3):
        await_bytes(first[a].slot(ALL, 0), first[a].far)
        for layer in PAIR:
            second[a][3].start(layer)
    last(DOWN, 0)
    last(GATE, 0)
    for n in range(4):
        for a in range(3):
            second[a][n].forward()
        if n == 1:
            up2(0)
            last(UP, 0)
    for a in (DOWN, GATE):
        near2(a)
        last(a, 1)
        last(a, 2)
    for n in range(1, 4):
        up2(n)
        last(UP, n)
    for a in (DOWN, GATE):
        far2(a)
        last(a, 3)

    for own, new in ((own_m, new_m), (own_v, new_v)):
        new[DOWN][...] = own[DOWN][...]
        for a in (GATE, UP):
            @pl.loop(0, ROWS)
            def _(r):
                for layer in PAIR:
                    for n in range(4):
                        new[a][r, layer : layer + 1, n * quarter : (n + 1) * quarter] = own[a][layer, pl.ds(n * ROWS + r, 1), :]

    for n in range(4):
        for a in range(3):
            third[a][n].forward()
    for n in range(4):
        for a in range(3):
            await_bytes(out[a].at[:, 0, :, 0:2] if a == DOWN else out[a].at[:, 0, 0:2], third[a][n].far)
    for a in range(3):
        for phase in range(3):
            sent(a, phase)
    await_bytes(parts.at[0:63], psem.at[0])


def write_kernel(*refs):
    *refs, sem = refs
    count = len(refs) // 2
    copies = []
    for n, (src, dst) in reversed(list(enumerate(zip(refs[:count], refs[count:])))):
        copies.append(pltpu.make_async_copy(src, dst, sem.at[n]))
        copies[-1].start()
    for copy in copies:
        copy.wait()


def solution(mesh):
    def step(*arrays):
        terms, weights, m, v = (arrays[i : i + 3] for i in (0, 3, 6, 9))
        cols, fcols = terms[GATE].shape[-1], terms[DOWN].shape[-1]
        rows, frows = terms[GATE].shape[-2], terms[DOWN].shape[-2]
        assert rows == 64 * ROWS and frows == 64 * TALL and cols % 512 == 0
        wide = lambda t: t.reshape(2, 4, 4, BLOCK, cols)
        tall = lambda t: t.reshape(2, 4, 4, 4, TALL, fcols)
        shaped = lambda three: (*map(wide, three[:DOWN]), tall(three[DOWN]))
        turn = lambda t: t.transpose(1, 0, 2)
        turned = lambda three: (*map(turn, three[:DOWN]), three[DOWN])
        stay = lambda t: pltpu.with_memory_space_constraint(t, pltpu.HBM)
        count = 2 * (2 * rows * cols + frows * fcols)
        anywhere, on_chip, off_chip = (pl.BlockSpec(memory_space=space) for space in (pl.ANY, pltpu.VMEM, pltpu.HBM))
        piece = (BLOCK, cols // 4)
        pieces = (piece, piece, (TALL, fcols))
        every = lambda dtype, *lead: [pltpu.VMEM((*lead, *p), dtype) for p in pieces]
        scratch = [*every(BF16, 2, 2, 4), *every(F32, 2, 2, 4), *every(BF16, 2, 4), *every(BF16, 2, 2, 4)]
        scratch += [*every(BF16, 2, 2), *every(F32, 2, 2), *every(BF16, 2), *every(BF16, 2, 2)]
        scratch += [*every(F32, 2), *every(F32, 2), *every(F32, 2)[:DOWN], every(BF16, 2)[DOWN], *every(F32, 2)]
        scratch += every(BF16, 2, 4, 4)[:DOWN]
        scratch += [pltpu.VMEM((64, cols // 4), F32), pltpu.VMEM((4, 64, cols // 4), F32), pltpu.VMEM((2, 2, BLOCK, cols), BF16)]
        scratch += [pltpu.VMEM((2, ROWS, 2, cols), F32)] * 2 + [pltpu.VMEM((64, 1, 128), F32)]
        scratch += [pltpu.SemaphoreType.DMA((n,)) for n in (9, 54, 12, 2)]
        ends = [(ROWS, 2, cols), (ROWS, 2, cols), (2, TALL, fcols)]
        big = [(2, 4, 4, BLOCK, cols), (2, 4, 4, BLOCK, cols), (2, 4, 4, 4, TALL, fcols)]
        made = pl.pallas_call(
            functools.partial(step_kernel, cols, count),
            out_shape=[pltpu.VMEM(s, BF16) for s in big] + [pltpu.VMEM(s, F32) for s in ends * 2],
            in_specs=[off_chip] * 12,
            out_specs=[on_chip] * 9,
            scratch_shapes=scratch,
            compiler_params=pltpu.CompilerParams(collective_id=0, has_side_effects=True, vmem_limit_bytes=STEP_MIB * MIB),
            name="step",
        )(*shaped([t[0] for t in terms]), *shaped(weights), *map(stay, (*turned(m), *turned(v))))
        outs = pl.pallas_call(
            write_kernel,
            out_shape=[jax.ShapeDtypeStruct(s, BF16) for s in big] + [jax.ShapeDtypeStruct(s, F32) for s in ends * 2],
            in_specs=[on_chip] * 9,
            out_specs=[anywhere] * 9,
            scratch_shapes=[pltpu.SemaphoreType.DMA((9,))],
            compiler_params=pltpu.CompilerParams(vmem_limit_bytes=2 * MIB),
            name="write",
        )(*made)
        news = tuple(one.reshape(w.shape) for one, w in zip(outs, weights))
        return (*news, *turned(outs[3:6]), *turned(outs[6:9]))

    all_of, cut = P(None, None, None), P(None, "dp", None)
    return jax.shard_map(
        step,
        mesh=mesh,
        in_specs=(P(("rep", "dp"), None, None, None),) * 3 + (all_of,) * 3 + (cut,) * 6,
        out_specs=(P("rep", None, None),) * 3 + (P("rep", "dp", None),) * 6,
        check_vma=False,
    )
```

time: 239 us -> 231 us (0.967)
  Pallas kernels: 238 us -> 230 us
    pallas_call x1, Pallas kernels: 228 us -> 220 us  [step(): pl.pallas_call(functools.partial(step_kernel, cols, count), out_shape=[pl...]
where the time goes in v4:
time: 231 us
  Pallas kernels  230 us (100%)
    pallas_call x1, Pallas kernels, step(): pl.pallas_call(functools.partial(step_kernel, cols, count), out_shape=[pl...  220 us
    pallas_call x1, Pallas kernels, step(): pl.pallas_call(write_kernel, out_shape=[jax.ShapeDtypeStruct(s, BF16) for...  10.1 us

profile of v4, /device:TPU:0, one launch (start us, length us, event | category | flops | bytes accessed | tf_op | source)
XLA Modules:
  0.0 230.5 jit_solution(14574356179502986615)
XLA Ops:
  0.6 219.8 %step.1 = (bf16[2,4,4,56,2560]{4,3,2,1,0:T(8,128)(2,1)S(1)}, bf16[2,4,4,56,2560]{4,3,2,1,0:T(8,128)(2,1)S(1)}, bf16[2,4,4,4,40,896]{5,4,3,2,1,0:T(8,128)(2,1)S(1...) custom-call(bf16[2,4,4,56,2560]{4,3,2,1,0:T(8,128)(2,1)} %bitcast.17, ...), custom_call_target="tpu_custom_call" | custom-call | tf_op jit(solution)/shard_map/step/pallas_call | solution.py:453
  220.4 10.1 %write.1 = (bf16[2,4,4,56,2560]{4,3,2,1,0:T(8,128)(2,1)}, bf16[2,4,4,56,2560]{4,3,2,1,0:T(8,128)(2,1)}, bf16[2,4,4,4,40,896]{5,4,3,2,1,0:T(8,128)(2,1)}, f32[14,...) custom-call(bf16[2,4,4,56,2560]{4,3,2,1,0:T(8,128)(2,1)S(1)} %get-tu, ...), custom_call_target="tpu_custom_call" | custom-call | tf_op jit(solution)/shard_map/write/pallas_call | solution.py:462

commit v5 on v4

--- a/solution.py
+++ b/solution.py
@@ -373,14 +373,13 @@
         await_bytes(first[a].slot(ALL, 0), first[a].far)
         for layer in PAIR:
             second[a][3].start(layer)
+    for n in range(4):
+        for a in (UP, GATE, DOWN):
+            second[a][n].forward()
     last(DOWN, 0)
     last(GATE, 0)
-    for n in range(4):
-        for a in range(3):
-            second[a][n].forward()
-        if n == 1:
-            up2(0)
-            last(UP, 0)
+    up2(0)
+    last(UP, 0)
     for a in (DOWN, GATE):
         near2(a)
         last(a, 1)

time: 231 us -> 223 us (0.965)
  Pallas kernels: 230 us -> 222 us
    pallas_call x1, Pallas kernels: 220 us -> 212 us  [step(): pl.pallas_call(functools.partial(step_kernel, cols, count), out_shape=[pl...]
where the time goes in v5:
time: 223 us
  Pallas kernels  222 us (100%)
    pallas_call x1, Pallas kernels, step(): pl.pallas_call(functools.partial(step_kernel, cols, count), out_shape=[pl...  212 us
    pallas_call x1, Pallas kernels, step(): pl.pallas_call(write_kernel, out_shape=[jax.ShapeDtypeStruct(s, BF16) for...  10.1 us

profile of v5, /device:TPU:0, one launch (start us, length us, event | category | flops | bytes accessed | tf_op | source)
XLA Modules:
  0.0 222.7 jit_solution(16004540373554279829)
XLA Ops:
  0.6 212.0 %step.1 = (bf16[2,4,4,56,2560]{4,3,2,1,0:T(8,128)(2,1)S(1)}, bf16[2,4,4,56,2560]{4,3,2,1,0:T(8,128)(2,1)S(1)}, bf16[2,4,4,4,40,896]{5,4,3,2,1,0:T(8,128)(2,1)S(1...) custom-call(bf16[2,4,4,56,2560]{4,3,2,1,0:T(8,128)(2,1)} %bitcast.17, ...), custom_call_target="tpu_custom_call" | custom-call | tf_op jit(solution)/shard_map/step/pallas_call | solution.py:452
  212.6 10.1 %write.1 = (bf16[2,4,4,56,2560]{4,3,2,1,0:T(8,128)(2,1)}, bf16[2,4,4,56,2560]{4,3,2,1,0:T(8,128)(2,1)}, bf16[2,4,4,4,40,896]{5,4,3,2,1,0:T(8,128)(2,1)}, f32[14,...) custom-call(bf16[2,4,4,56,2560]{4,3,2,1,0:T(8,128)(2,1)S(1)} %get-tu, ...), custom_call_target="tpu_custom_call" | custom-call | tf_op jit(solution)/shard_map/write/pallas_call | solution.py:461
